TPU v7x, 32 devices: a whole 2x2x4 slice. The times are simulated.
32 devices in a mesh: ens: 4 (over y, x), slab: 8 (over z, core).
Axes of the slice: x: 2, y: 2, z: 4, core: 2. Of those that a mesh axis runs over, the one named last changes fastest.
Arguments:
- velocity: float32 [4, 3, 8, 2048, 1024], P('ens', None, None, 'slab'), may hold values from -6 to 6
- cutoffs: int32 [4, 2, 8], P('ens'), may hold values from 128 to 511, as said below
- plane_index: int32 [4], P('ens'), may hold values from 0 to 2047
- boundary_index: int32 [4], P('ens'), may hold values from 0 to 2047
Outputs:
- blended: float32 [4, 3, 8, 2048, 1024], P('ens', None, None, 'slab')
Inputs may be any that keep to these rules, and one draw needn't show every extreme that they name: `cutoffs`: row 0 lies in 256 to 511 and row 1 in 128 to 255; in every member some level has row 0 equal to 511 and some level has row 1 equal to 255.
All inputs are finite; a program needn't handle non-finite values.
Results may differ from a plain program's by a relative error of at most 0.0003.
Values sent between devices are 32-bit elements; how exact they have to be, the bound alone decides.
A program may use at most 128 MiB of HBM per device.

v0:
```python
import math
import jax
import jax.numpy as jnp
from jax import lax
from jax.sharding import PartitionSpec as P

KX = 512
KY = 256
highest = lax.Precision.HIGHEST


def spread(value, axis, source):
    kept = jnp.where(lax.axis_index(axis) == source, value, 0).astype(value.dtype)
    return lax.psum(kept, axis)


def shifted(block, axis, distance):
    devices = range(lax.axis_size(axis))
    route = [((i - distance) % len(devices), i) for i in devices]
    return lax.ppermute(block, axis, route)


def basis_pair(length, mode_count):
    position = jnp.arange(length, dtype=jnp.int32)
    wavenum = jnp.arange(mode_count, dtype=jnp.int32)
    angles = (position[:, None] * wavenum[None, :] % length).astype(jnp.float32) * (
        2.0 * math.pi / length
    )
    basis_cols = jnp.concatenate([jnp.cos(angles), jnp.sin(angles)], axis=1)
    weight = jnp.where(wavenum == 0, 1.0, 2.0).astype(jnp.float32) / length
    weight = jnp.concatenate([weight, weight])
    return (basis_cols * weight[None, :], basis_cols.T)


def mode_keep(levels_cut, mode_count):
    wavenum = jnp.tile(jnp.arange(mode_count, dtype=jnp.int32), 2)
    return (wavenum[None, :] <= levels_cut[:, None]).astype(jnp.float32)


def x_filter(columns, analysis_x, synthesis_x, keep_x):
    coeffs = (
        jnp.einsum("xk,czxj->czkj", analysis_x, columns, precision=highest)
        * keep_x[None, :, :, None]
    )
    return jnp.einsum("kx,czkj->czxj", synthesis_x, coeffs, precision=highest)


def on_device(velocity, cutoffs, plane_index, boundary_index):
    devices = lax.axis_size("slab")
    member_rows = velocity.shape[3]
    across = velocity.shape[4]
    along = member_rows * devices
    analysis_x, synthesis_x = basis_pair(along, KX)
    analysis_y, synthesis_y = basis_pair(across, KY)
    keep_x = mode_keep(cutoffs[0, 0], KX)
    keep_y = mode_keep(cutoffs[0, 1], KY)
    own_field = velocity[0]
    spectra = (
        jnp.einsum("czxy,yj->czxj", own_field, analysis_y, precision=highest)
        * keep_y[None, :, None, :]
    )
    columns = lax.all_to_all(spectra, "slab", split_axis=3, concat_axis=2, tiled=True)
    smooth = x_filter(columns, analysis_x, synthesis_x, keep_x)
    returned = lax.all_to_all(smooth, "slab", split_axis=2, concat_axis=3, tiled=True)
    result = jnp.einsum("czxj,jy->czxy", returned, synthesis_y, precision=highest)
    first_row = lax.axis_index("slab") * member_rows
    local_index = jnp.clip(plane_index[0] - first_row, 0, member_rows - 1)
    plane_part = lax.dynamic_index_in_dim(result, local_index, 2, keepdims=False)
    source_plane = spread(plane_part, "slab", plane_index[0] // member_rows)
    inflow = shifted(source_plane, "ens", 1)
    streamwise = first_row + jnp.arange(member_rows, dtype=jnp.int32)
    offset = jnp.abs(streamwise - boundary_index[0])
    distance = jnp.minimum(offset, along - offset)
    relax = jnp.exp(-distance.astype(jnp.float32) / (along / 4.0))
    weight = relax[None, None, :, None]
    blended = result + weight * (inflow[:, :, None, :] - result)
    return blended[None]


def solution(mesh):
    in_specs = (P("ens", None, None, "slab", None), P("ens", None, None), P("ens"), P("ens"))
    out_specs = P("ens", None, None, "slab", None)
    return jax.shard_map(
        on_device, mesh=mesh, in_specs=in_specs, out_specs=out_specs, check_vma=False
    )
```

profile of v0, /device:TPU:8, one launch (start us, length us, event | category | flops | bytes accessed | tf_op | source)
XLA Modules:
  0.0 1089.4 jit_solution(2496585179114449928)
XLA Ops:
  6.5 4.1 fusion.37
  10.7 0.8 slice_bitcast_fusion
  11.4 0.1 compare_convert_fusion.1
  11.5 84.5 %bitcast_multiply_fusion = f32[3,8,256,512]{2,3,1,0:T(8,128)} fusion(f32[8,512]{1,0:T(8,128)S(1)} %compare_convert_fusion.1, f32[1,3,8,256,1024]{4,3,2,1,0:T(8,128)} %param.4, f32[1024,256]{1,0:T(8,128)S(1)} %get-tuple-element.7, f32[1024,256]{1,0:T(8,128)S(1)} %get-tuple-element.8, f32[512]{0:T(512)S(1)} %pad_maximum_fusion.7), kind=kOutput, calls=%fused_computation.3 | convolution fusion | flops 38658899968 | bytes 39864320 | tf_op jit(solution)/shard_map/czxy,yj->czxj/dot_general | solution.py:59
  96.0 16.3 %copy.17 = f32[3,8,256,512]{2,1,0,3:T(8,128)} copy(f32[3,8,256,512]{2,3,1,0:T(8,128)} %bitcast_multiply_fusion) | data formatting | bytes 25165824 | tf_op jit(solution)/shard_map/mul | solution.py:59
  112.3 5.5 all-to-all-start
  117.9 0.1 compare_convert_fusion
  118.0 17.5 %fusion.27 = (f32[2048,512]{1,0:T(8,128)}, f32[2048,512]{1,0:T(8,128)}) fusion(), kind=kLoop, calls=%fused_computation.29 | loop fusion | flops 14680064 | bytes 8388608 | tf_op jit(solution)/shard_map/sin | solution.py:29
  135.6 252.6 %all-to-all-done = f32[3,8,256,512]{2,1,0,3:T(8,128)} async-done(((f32[3,8,256,512]{2,1,0,3:T(8,128)}), f32[3,8,256,512]{2,1,0,3:T(8,128)}, u32[]{:S(2)}, u32[]{:S(2)}) %all-to-all-start) | async-done | bytes 12582944 | tf_op jit(solution)/shard_map/all_to_all | solution.py:62
  388.1 16.6 %copy.36 = f32[3,8,256,8,64]{2,3,4,1,0:T(8,128)} copy(f32[3,8,256,8,64]{2,1,0,4,3:T(8,128)} %bitcast.4) | data formatting | bytes 25165824 | tf_op jit(solution)/shard_map/all_to_all | solution.py:62
  404.8 13.6 %all_to_all.29 = f32[3,8,2048,64]{2,3,1,0:T(8,128)} reshape(f32[3,8,8,256,64]{3,2,4,1,0:T(8,128)} %bitcast.77) | data formatting | bytes 25165824 | tf_op jit(solution)/shard_map/all_to_all | solution.py:62
  418.4 0.0 copy-start.1
  418.4 0.0 copy-start.2
  418.4 47.2 %fusion.4 = f32[3,8,64,1024]{3,2,1,0:T(8,128)} fusion(f32[3,8,2048,64]{2,3,1,0:T(8,128)} %all_to_all.29, f32[2048,512]{1,0:T(8,128)} %get-tuple-element.9, f32[2048,512]{1,0:T(8,128)} %get-tuple-element.10, f32[1024]{0:T(1024)S(1)} %pad_maximum_fusion.6), kind=kOutput, calls=%fused_computation.8 | convolution fusion | flops 38658899968 | bytes 27267072 | tf_op jit(solution)/shard_map/xk,czxj->czkj/dot_general | solution.py:42
  465.6 0.0 copy-done.1
  465.6 0.0 copy-done.2
  465.6 44.3 %fusion.9 = f32[3,8,2048,64]{2,3,1,0:T(8,128)} fusion(f32[2048,512]{1,0:T(8,128)S(1)} %copy-done.1, f32[2048,512]{1,0:T(8,128)S(1)} %copy-done.2, f32[3,8,64,1024]{3,2,1,0:T(8,128)} %fusion.4, f32[8,1024]{1,0:T(8,128)S(1)} %compare_convert_fusion), kind=kOutput, calls=%fused_computation.16 | convolution fusion | flops 38658375680 | bytes 27295744 | tf_op jit(solution)/shard_map/kx,czkj->czxj/dot_general | solution.py:45
  509.9 17.7 %copy.19 = f32[3,8,2048,64]{3,1,0,2:T(8,128)} copy(f32[3,8,2048,64]{2,3,1,0:T(8,128)} %fusion.9) | data formatting | bytes 25165824 | tf_op jit(solution)/shard_map/kx,czkj->czxj/transpose | solution.py:45
  527.6 20.5 %reshape.91 = f32[8,1,393216]{2,1,0:T(1,128)} reshape(f32[2048,3,8,64]{3,2,1,0:T(8,128)} %bitcast.74) | data formatting | bytes 25165824
  548.1 8.8 all-to-all-start.1
  556.9 0.0 all-reduce.2.cloned.1.call-start
  557.6 269.6 %all-to-all-done.1 = f32[8,1,393216]{2,1,0:T(1,128)} async-done(((f32[8,1,393216]{2,1,0:T(1,128)}), f32[8,1,393216]{2,1,0:T(1,128)}, u32[]{:S(2)}, u32[]{:S(2)}) %all-to-all-start.1) | async-done | bytes 12582944 | tf_op jit(solution)/shard_map/all_to_all | solution.py:64
  827.2 0.5 broadcast.88
  827.7 36.8 %reduce = f32[8,393216]{1,0:T(8,128)} reduce(f32[8,1,393216]{2,1,0:T(1,128)} %all-to-all-done.1, f32[]{:T(128)} %broadcast.88), dimensions={1}, to_apply=%all_to_all.30.reduce_sub_computation | reduce | bytes 25165828 | tf_op jit(solution)/shard_map/all_to_all | solution.py:64
  864.5 23.2 %reshape.92 = f32[2048,3,8,64]{3,2,1,0:T(8,128)} reshape(f32[8,393216]{1,0:T(8,128)} %reduce) | data formatting | bytes 25165824
  887.7 18.7 %copy.21 = f32[3,8,256,8,64]{2,4,3,1,0:T(8,128)} copy(f32[3,8,256,8,64]{4,1,0,2,3:T(8,128)} %bitcast.75) | data formatting | bytes 25165824 | tf_op jit(solution)/shard_map/all_to_all | solution.py:64
  906.4 85.2 %fusion.24 = f32[3,8,256,1024]{3,2,1,0:T(8,128)S(1)} fusion(f32[3,8,256,512]{2,3,1,0:T(8,128)} %bitcast.76, f32[1024,256]{1,0:T(8,128)S(1)} %get-tuple-element.7, f32[1024,256]{1,0:T(8,128)S(1)} %get-tuple-element.8), kind=kOutput, calls=%fused_computation.26 | convolution fusion | flops 38655229952 | bytes 39845888 | tf_op jit(solution)/shard_map/czxj,jy->czxy/dot_general | solution.py:65
  991.5 0.0 copy-start
  991.6 8.9 copy-done
  1000.5 0.1 broadcast_select_fusion
  1000.6 0.7 copy.37
  1001.2 0.0 all-reduce.2.cloned.1.call-update
  1001.9 55.8 %all-reduce.2.cloned.1.call-done = f32[3,8,1024]{2,1,0:T(8,128)} async-done(((f32[3,8,1024]{2,1,0:T(8,128)}), f32[3,8,1024]{2,1,0:T(8,128)}) %all-reduce.2.cloned.1.call-update) | async-done | bytes 98320 | tf_op jit(solution)/shard_map/psum | solution.py:14
  1057.7 1.5 collective-permute-start
  1059.2 4.2 collective-permute-done
  1063.4 18.8 %add_bitcast_fusion = f32[1,3,8,256,1024]{4,3,2,1,0:T(8,128)} fusion(f32[3,8,256,1024]{3,2,1,0:T(8,128)} %copy-done, f32[3,8,1024]{2,1,0:T(8,128)S(1)} %collective-permute-done, f32[256]{0:T(256)S(1)} %fusion.42), kind=kLoop, calls=%fused_computation.2 | loop fusion | flops 18874368 | bytes 50430976 | tf_op jit(solution)/shard_map/broadcast_in_dim | solution.py:77
  (9 shorter events, 0.1 us)
Async XLA Ops:
  112.3 275.8 %all-to-all-start = ((f32[3,8,256,512]{2,1,0,3:T(8,128)}), f32[3,8,256,512]{2,1,0,3:T(8,128)}, u32[]{:S(2)}, u32[]{:S(2)}) async-start(f32[3,8,256,512]{2,1,0,3:T(8,128)} %copy.17), calls=%async_computation | async-start | bytes 25165824 | tf_op jit(solution)/shard_map/all_to_all | solution.py:62
  418.4 47.2 %copy-start.1 = (f32[2048,512]{1,0:T(8,128)S(1)}, f32[2048,512]{1,0:T(8,128)}, u32[]{:S(2)}) copy-start(f32[2048,512]{1,0:T(8,128)} %get-tuple-element.9) | copy-start | bytes 12582916
  418.4 47.2 %copy-start.2 = (f32[2048,512]{1,0:T(8,128)S(1)}, f32[2048,512]{1,0:T(8,128)}, u32[]{:S(2)}) copy-start(f32[2048,512]{1,0:T(8,128)} %get-tuple-element.10) | copy-start | bytes 12582916
  548.1 279.1 %all-to-all-start.1 = ((f32[8,1,393216]{2,1,0:T(1,128)}), f32[8,1,393216]{2,1,0:T(1,128)}, u32[]{:S(2)}, u32[]{:S(2)}) async-start(f32[8,1,393216]{2,1,0:T(1,128)} %reshape.91), calls=%async_computation.1 | async-start | bytes 25165824 | tf_op jit(solution)/shard_map/all_to_all | solution.py:64
  556.9 500.8 %all-reduce.2.cloned.1.call-start = ((), (), s32[]{:S(2)}) async-start(), calls=%async_computation.2 | async-start | bytes 196608 | tf_op jit(solution)/shard_map/psum | solution.py:14
  991.5 8.9 copy-start
  1057.7 5.7 collective-permute-start
Sparse Core Ops, SparseCore 0:
  1001.4 56.2 all-reduce.1
where the time goes:
time: 1090 us
  waiting for transfers between devices  582 us (53%)
  matrix products  261 us (24%)
  local copies, waits for them, and re-layouts  138 us (13%)
  other arithmetic  77.5 us (7%)
  starting transfers between devices  15.8 us (1%)
  between operations  15.2 us (1%)
    all_to_all x1, waiting for transfers between devices, on_device(): lax.all_to_all(smooth, 'slab', split_axis=2, concat_axis=3, tiled=True)  270 us
    all_to_all x1, waiting for transfers between devices, on_device(): lax.all_to_all(spectra, 'slab', split_axis=3, concat_axis=2, tiled=True)  253 us
    dot_general x1, matrix products, on_device(): jnp.einsum('czxj,jy->czxy', returned, synthesis_y, precision=highest)  85.2 us
    dot_general x1, matrix products, on_device(): jnp.einsum('czxy,yj->czxj', own_field, analysis_y, precision=highest)  84.5 us
    psum x1, waiting for transfers between devices, spread(): return lax.psum(kept, axis)  55.8 us
    unnamed x13, local copies, waits for them, and re-layouts  53.3 us
    dot_general x1, matrix products, x_filter(): jnp.einsum('xk,czxj->czkj', analysis_x, columns, precision=highest)  47.2 us
    dot_general x1, matrix products, x_filter(): return jnp.einsum('kx,czkj->czxj', synthesis_x, coeffs, precision=highest)  44.3 us
  transfers between devices with their start and end apart: 4, of which 4 were waited for; matrix products, arithmetic and copies ran while one was open for 2% of the time, Pallas kernels for 0%

commit v1 on v0

--- a/solution.py
+++ b/solution.py
@@ -11,7 +11,7 @@
 
 def spread(value, axis, source):
     kept = jnp.where(lax.axis_index(axis) == source, value, 0).astype(value.dtype)
-    return lax.psum(kept, axis)
+    return jnp.sum(lax.all_gather(kept, axis), axis=0)
 
 
 def shifted(block, axis, distance):

time: 1090 us -> 1060 us (0.972)
  waiting for transfers between devices: 582 us -> 526 us
  blocking collectives: 0 us -> 16.4 us
  matrix products: 261 us -> 275 us
  between operations: 15.2 us -> 1.62 us
    psum x1 -> x0, waiting for transfers between devices: 55.8 us -> none  [spread(): return lax.psum(kept, axis)]
    all_gather x0 -> x1, blocking collectives: none -> 16.4 us  [spread(): return jnp.sum(lax.all_gather(kept, axis), axis=0)]
    dot_general x1, matrix products: 85.2 us -> 99.6 us  [on_device(): jnp.einsum('czxj,jy->czxy', returned, synthesis_y, precision=highest)]
    unnamed x13 -> x12, local copies, waits for them, and re-layouts: 53.3 us -> 52.7 us
  transfers between devices with their start and end apart: 4 -> 3, of which waited for: 4 -> 3; matrix products, arithmetic and copies ran while one was open for 2% -> 2% of each run, Pallas kernels for 0% -> 0%
where the time goes in v1:
time: 1060 us; the launch traced here: 1050 us
  waiting for transfers between devices  526 us (50%)
  matrix products  275 us (26%)
  local copies, waits for them, and re-layouts  137 us (13%)
  other arithmetic  77.3 us (7%)
  blocking collectives  16.4 us (2%)
  starting transfers between devices  16.2 us (2%)
    all_to_all x1, waiting for transfers between devices, on_device(): lax.all_to_all(smooth, 'slab', split_axis=2, concat_axis=3, tiled=True)  269 us
    all_to_all x1, waiting for transfers between devices, on_device(): lax.all_to_all(spectra, 'slab', split_axis=3, concat_axis=2, tiled=True)  253 us
    dot_general x1, matrix products, on_device(): jnp.einsum('czxj,jy->czxy', returned, synthesis_y, precision=highest)  99.6 us
    dot_general x1, matrix products, on_device(): jnp.einsum('czxy,yj->czxj', own_field, analysis_y, precision=highest)  84.4 us
    unnamed x12, local copies, waits for them, and re-layouts  52.7 us
    dot_general x1, matrix products, x_filter(): jnp.einsum('xk,czxj->czkj', analysis_x, columns, precision=highest)  47.2 us
    dot_general x1, matrix products, x_filter(): return jnp.einsum('kx,czkj->czxj', synthesis_x, coeffs, precision=highest)  44.3 us
    all_to_all x1, other arithmetic, on_device(): lax.all_to_all(smooth, 'slab', split_axis=2, concat_axis=3, tiled=True)  36.6 us
  transfers between devices with their start and end apart: 3, of which 3 were waited for; matrix products, arithmetic and copies ran while one was open for 2% of the time, Pallas kernels for 0%

profile of v1, /device:TPU:8, one launch (start us, length us, event | category | flops | bytes accessed | tf_op | source)
XLA Modules:
  0.0 1049.9 jit_solution(16726689763349839345)
XLA Ops:
  0.0 4.1 fusion.37
  4.1 0.8 slice_bitcast_fusion
  4.9 0.1 compare_convert_fusion.1
  5.0 84.4 %bitcast_multiply_fusion = f32[3,8,256,512]{2,3,1,0:T(8,128)} fusion(f32[8,512]{1,0:T(8,128)S(1)} %compare_convert_fusion.1, f32[1,3,8,256,1024]{4,3,2,1,0:T(8,128)} %param.4, f32[1024,256]{1,0:T(8,128)S(1)} %get-tuple-element.7, f32[1024,256]{1,0:T(8,128)S(1)} %get-tuple-element.8, f32[512]{0:T(512)S(1)} %pad_maximum_fusion.7), kind=kOutput, calls=%fused_computation.3 | convolution fusion | flops 38658899968 | bytes 39864320 | tf_op jit(solution)/shard_map/czxy,yj->czxj/dot_general | solution.py:59
  89.4 16.3 %copy.18 = f32[3,8,256,512]{2,1,0,3:T(8,128)} copy(f32[3,8,256,512]{2,3,1,0:T(8,128)} %bitcast_multiply_fusion) | data formatting | bytes 25165824 | tf_op jit(solution)/shard_map/mul | solution.py:59
  105.7 5.5 all-to-all-start
  111.3 0.1 compare_convert_fusion
  111.4 17.5 %fusion.27 = (f32[2048,512]{1,0:T(8,128)}, f32[2048,512]{1,0:T(8,128)}) fusion(), kind=kLoop, calls=%fused_computation.29 | loop fusion | flops 14680064 | bytes 8388608 | tf_op jit(solution)/shard_map/sin | solution.py:29
  128.9 252.6 %all-to-all-done = f32[3,8,256,512]{2,1,0,3:T(8,128)} async-done(((f32[3,8,256,512]{2,1,0,3:T(8,128)}), f32[3,8,256,512]{2,1,0,3:T(8,128)}, u32[]{:S(2)}, u32[]{:S(2)}) %all-to-all-start) | async-done | bytes 12582944 | tf_op jit(solution)/shard_map/all_to_all | solution.py:62
  381.5 16.6 %copy.36 = f32[3,8,256,8,64]{2,3,4,1,0:T(8,128)} copy(f32[3,8,256,8,64]{2,1,0,4,3:T(8,128)} %bitcast.4) | data formatting | bytes 25165824 | tf_op jit(solution)/shard_map/all_to_all | solution.py:62
  398.1 13.6 %all_to_all.29 = f32[3,8,2048,64]{2,3,1,0:T(8,128)} reshape(f32[3,8,8,256,64]{3,2,4,1,0:T(8,128)} %bitcast.75) | data formatting | bytes 25165824 | tf_op jit(solution)/shard_map/all_to_all | solution.py:62
  411.8 0.0 copy-start.1
  411.8 0.0 copy-start.2
  411.8 47.2 %fusion.4 = f32[3,8,64,1024]{3,2,1,0:T(8,128)} fusion(f32[3,8,2048,64]{2,3,1,0:T(8,128)} %all_to_all.29, f32[2048,512]{1,0:T(8,128)} %get-tuple-element.9, f32[2048,512]{1,0:T(8,128)} %get-tuple-element.10, f32[1024]{0:T(1024)S(1)} %pad_maximum_fusion.6), kind=kOutput, calls=%fused_computation.8 | convolution fusion | flops 38658899968 | bytes 27267072 | tf_op jit(solution)/shard_map/xk,czxj->czkj/dot_general | solution.py:42
  459.0 0.0 copy-done.1
  459.0 0.0 copy-done.2
  459.0 44.3 %fusion.9 = f32[3,8,2048,64]{2,3,1,0:T(8,128)} fusion(f32[2048,512]{1,0:T(8,128)S(1)} %copy-done.1, f32[2048,512]{1,0:T(8,128)S(1)} %copy-done.2, f32[3,8,64,1024]{3,2,1,0:T(8,128)} %fusion.4, f32[8,1024]{1,0:T(8,128)S(1)} %compare_convert_fusion), kind=kOutput, calls=%fused_computation.16 | convolution fusion | flops 38658375680 | bytes 27295744 | tf_op jit(solution)/shard_map/kx,czkj->czxj/dot_general | solution.py:45
  503.2 17.9 %copy.20 = f32[3,8,2048,64]{3,1,0,2:T(8,128)} copy(f32[3,8,2048,64]{2,3,1,0:T(8,128)} %fusion.9) | data formatting | bytes 25165824 | tf_op jit(solution)/shard_map/kx,czkj->czxj/transpose | solution.py:45
  521.2 20.5 %reshape.102 = f32[8,1,393216]{2,1,0:T(1,128)} reshape(f32[2048,3,8,64]{3,2,1,0:T(8,128)} %bitcast.72) | data formatting | bytes 25165824
  541.6 8.8 all-to-all-start.1
  551.7 269.0 %all-to-all-done.1 = f32[8,1,393216]{2,1,0:T(1,128)} async-done(((f32[8,1,393216]{2,1,0:T(1,128)}), f32[8,1,393216]{2,1,0:T(1,128)}, u32[]{:S(2)}, u32[]{:S(2)}) %all-to-all-start.1) | async-done | bytes 12582944 | tf_op jit(solution)/shard_map/all_to_all | solution.py:64
  820.7 0.5 broadcast.102
  821.2 36.6 %reduce = f32[8,393216]{1,0:T(8,128)} reduce(f32[8,1,393216]{2,1,0:T(1,128)} %all-to-all-done.1, f32[]{:T(128)} %broadcast.102), dimensions={1}, to_apply=%all_to_all.30.reduce_sub_computation | reduce | bytes 25165828 | tf_op jit(solution)/shard_map/all_to_all | solution.py:64
  857.8 23.2 %reshape.103 = f32[2048,3,8,64]{3,2,1,0:T(8,128)} reshape(f32[8,393216]{1,0:T(8,128)} %reduce) | data formatting | bytes 25165824
  881.1 18.6 %copy.22 = f32[3,8,256,8,64]{2,4,3,1,0:T(8,128)} copy(f32[3,8,256,8,64]{4,1,0,2,3:T(8,128)} %bitcast.73) | data formatting | bytes 25165824 | tf_op jit(solution)/shard_map/all_to_all | solution.py:64
  899.7 99.6 %fusion.24 = f32[3,8,256,1024]{3,2,1,0:T(8,128)S(1)} fusion(f32[3,8,256,512]{2,3,1,0:T(8,128)} %bitcast.74, f32[1024,256]{1,0:T(8,128)S(1)} %get-tuple-element.7, f32[1024,256]{1,0:T(8,128)S(1)} %get-tuple-element.8), kind=kOutput, calls=%fused_computation.26 | convolution fusion | flops 38655229952 | bytes 39845888 | tf_op jit(solution)/shard_map/czxj,jy->czxy/dot_general | solution.py:65
  999.3 0.0 copy-start
  999.3 8.9 copy-done
  1008.2 0.1 broadcast_select_fusion
  1008.3 16.4 %all-gather = f32[24,8,1,1024]{3,1,2,0:T(8,128)S(1)} all-gather(f32[3,8,1,1024]{3,1,2,0:T(8,128)S(1)} %copy.24), channel_id=2, replica_groups=mesh['ens'=4,'slab'=8] {'slab'}, dimensions={0}, use_global_device_ids=true | all-gather | bytes 884736 | tf_op jit(solution)/shard_map/all_gather | solution.py:14
  1024.7 1.9 collective-permute-start
  1026.7 4.2 collective-permute-done
  1030.9 18.8 %add_bitcast_fusion = f32[1,3,8,256,1024]{4,3,2,1,0:T(8,128)} fusion(f32[3,8,256,1024]{3,2,1,0:T(8,128)} %copy-done, f32[3,8,1024]{2,1,0:T(8,128)S(1)} %collective-permute-done, f32[256]{0:T(256)S(1)} %fusion.42), kind=kLoop, calls=%fused_computation.2 | loop fusion | flops 18874368 | bytes 50430976 | tf_op jit(solution)/shard_map/broadcast_in_dim | solution.py:77
  (11 shorter events, 0.1 us)
Async XLA Ops:
  105.7 275.8 %all-to-all-start = ((f32[3,8,256,512]{2,1,0,3:T(8,128)}), f32[3,8,256,512]{2,1,0,3:T(8,128)}, u32[]{:S(2)}, u32[]{:S(2)}) async-start(f32[3,8,256,512]{2,1,0,3:T(8,128)} %copy.18), calls=%async_computation | async-start | bytes 25165824 | tf_op jit(solution)/shard_map/all_to_all | solution.py:62
  411.8 47.2 %copy-start.1 = (f32[2048,512]{1,0:T(8,128)S(1)}, f32[2048,512]{1,0:T(8,128)}, u32[]{:S(2)}) copy-start(f32[2048,512]{1,0:T(8,128)} %get-tuple-element.9) | copy-start | bytes 12582916
  411.8 47.2 %copy-start.2 = (f32[2048,512]{1,0:T(8,128)S(1)}, f32[2048,512]{1,0:T(8,128)}, u32[]{:S(2)}) copy-start(f32[2048,512]{1,0:T(8,128)} %get-tuple-element.10) | copy-start | bytes 12582916
  541.6 279.1 %all-to-all-start.1 = ((f32[8,1,393216]{2,1,0:T(1,128)}), f32[8,1,393216]{2,1,0:T(1,128)}, u32[]{:S(2)}, u32[]{:S(2)}) async-start(f32[8,1,393216]{2,1,0:T(1,128)} %reshape.102), calls=%async_computation.1 | async-start | bytes 25165824 | tf_op jit(solution)/shard_map/all_to_all | solution.py:64
  999.3 8.9 copy-start
  1024.7 6.2 collective-permute-start
